TPU v7x, 32 devices: a whole 2x2x4 slice. The times are simulated.
32 devices in a mesh: layer: 8 (over z, x), rep: 4 (over y, core).
Axes of the slice: x: 2, y: 2, z: 4, core: 2. Of those that a mesh axis runs over, the one named last changes fastest.
Arguments:
- inverse_root: bfloat16 [64, 16, 128, 128], P('layer', 'rep'), may hold values from -0.625 to 0.625
- square_root: bfloat16 [64, 16, 128, 128], P('layer', 'rep'), may hold values from -0.625 to 0.625
- pattern: int32 [64, 16], P('layer', 'rep'), may hold values from 0 to 1, as said below
Outputs:
- inverse_next: bfloat16 [64, 16, 128, 128], P('layer', 'rep')
- square_next: bfloat16 [64, 16, 128, 128], P('layer', 'rep')
Inputs may be any that keep to these rules, and one draw needn't show every extreme that they name: 1 marks a tile of the common pattern. Slot 8 is 1 in every block row, and slot w of block row i is 0 where i - 8 + w lies outside 0 to 63.
All inputs are finite; a program needn't handle non-finite values.
Results may differ from a plain program's by a relative error of at most 0.018.
Values may be sent and summed in bfloat16 or wider, within the bound.
A program may use at most 128 MiB of HBM per device.

v0:
```python
import jax
import jax.numpy as jnp
from jax import lax
from jax.sharding import PartitionSpec as P


def passed_along(block, axis, distance):
    devices = range(lax.axis_size(axis))
    route = [(i - distance, i) for i in devices if i - distance in devices]
    return lax.ppermute(block, axis, route)


def band_product(left_tiles, right_tiles):
    row_count = left_tiles.shape[0]
    slot_count = left_tiles.shape[1]
    groups = lax.axis_size("rep")
    band_slots = slot_count * groups
    half_band = band_slots // 2
    window_rows = row_count + slot_count - 1
    depth_rows = -(-half_band // row_count)
    offsets = list(range(depth_rows, 0, -1)) + list(range(-1, -depth_rows - 1, -1))
    shifted = [passed_along(right_tiles, "layer", shift_by) for shift_by in offsets]
    extended = jnp.concatenate(shifted[:depth_rows] + [right_tiles] + shifted[depth_rows:], axis=0)
    first_row = depth_rows * row_count - half_band
    row_index = (
        first_row
        + jnp.arange(groups, dtype=jnp.int32)[:, None] * slot_count
        + jnp.arange(window_rows, dtype=jnp.int32)[None, :]
    )
    outgoing = jnp.take(extended, row_index, axis=0)
    incoming = lax.all_to_all(outgoing, "rep", split_axis=0, concat_axis=2, tiled=True)[0]
    replica = lax.axis_index("rep")
    wide_span = band_slots + slot_count - 1
    tile_size = left_tiles.shape[2]
    summed = jnp.zeros((row_count, wide_span, tile_size, tile_size), jnp.float32)
    for local_slot in range(slot_count):
        product = jnp.einsum(
            "iab,ivbc->ivac",
            left_tiles[:, local_slot],
            incoming[local_slot : local_slot + row_count],
            preferred_element_type=jnp.float32,
        )
        summed = summed + jnp.pad(
            product, ((0, 0), (local_slot, slot_count - 1 - local_slot), (0, 0), (0, 0))
        )
    padded = jnp.pad(summed, ((0, 0), (band_slots, band_slots), (0, 0), (0, 0)))
    offset = band_slots + half_band - replica * slot_count
    partial_value = lax.dynamic_slice_in_dim(padded, offset, band_slots, axis=1)
    return lax.psum_scatter(
        partial_value.astype(jnp.bfloat16), "rep", scatter_dimension=1, tiled=True
    ).astype(jnp.float32)


def body(inverse_root, square_root, pattern):
    in_pattern = (pattern == 1)[:, :, None, None]
    inverse_kept = jnp.where(in_pattern, inverse_root, jnp.zeros_like(inverse_root))
    square_kept = jnp.where(in_pattern, square_root, jnp.zeros_like(square_root))
    intersection = jnp.where(in_pattern, band_product(inverse_kept, square_kept), jnp.float32(0.0))
    slot_count = pattern.shape[1]
    half_band = slot_count * lax.axis_size("rep") // 2
    slot_ids = lax.axis_index("rep") * slot_count + jnp.arange(slot_count, dtype=jnp.int32)
    diagonal = (slot_ids == half_band).astype(jnp.float32)
    identity = jnp.eye(inverse_root.shape[2], dtype=jnp.float32)
    update = jnp.where(
        in_pattern,
        1.5 * diagonal[None, :, None, None] * identity - 0.5 * intersection,
        jnp.float32(0.0),
    ).astype(jnp.bfloat16)
    square_next = jnp.where(in_pattern, band_product(square_kept, update), jnp.float32(0.0)).astype(
        jnp.bfloat16
    )
    inverse_next = jnp.where(
        in_pattern, band_product(update, inverse_kept), jnp.float32(0.0)
    ).astype(jnp.bfloat16)
    return (inverse_next, square_next)


def solution(mesh):
    placed = (P("layer", "rep", None, None), P("layer", "rep", None, None), P("layer", "rep"))
    return jax.shard_map(
        body,
        mesh=mesh,
        in_specs=placed,
        out_specs=(P("layer", "rep", None, None), P("layer", "rep", None, None)),
        check_vma=False,
    )
```

profile of v0, /device:TPU:17, one launch (start us, length us, event | category | flops | bytes accessed | tf_op | source)
XLA Modules:
  0.0 668.2 jit_solution(13496988569349193323)
XLA Ops:
  17.0 41.0 %collective-permute-done.2 = bf16[8,4,128,128]{3,2,0,1:T(8,128)(2,1)S(1)} collective-permute-done((bf16[8,4,128,128]{3,2,0,1:T(8,128)(2,1)S(1)}, bf16[8,4,128,128]{3,2,0,1:T(8,128)(2,1)S(1)}, u32[]{:S(2)}, u32[]{:S(2)}) %collective-permute-start.2) | collective-permute-done | bytes 1048608 | tf_op jit(solution)/shard_map/ppermute | solution.py:10
  79.4 63.9 %all-to-all-done.1 = bf16[4,11,4,128,128]{4,3,2,1,0:T(8,128)(2,1)} async-done(((bf16[4,11,4,128,128]{4,3,2,1,0:T(8,128)(2,1)}), bf16[4,11,4,128,128]{4,3,2,1,0:T(8,128)(2,1)}, u32[]{:S(2)}, u32[]{:S(2)}) %all-to-all-start.1) | async-done | bytes 5767200 | tf_op jit(solution)/shard_map/all_to_all | solution.py:31
  143.4 12.2 %fusion.66 = (bf16[1,8,4,4,128,128]{5,4,3,1,2,0:T(8,128)(2,1)}, bf16[1,8,4,4,128,128]{5,4,3,1,2,0:T(8,128)(2,1)}, bf16[1,8,4,4,128,128]{5,4,3,1,2,0:T(8,128)(2,1)}, bf16[1,8,4,4,128,128]{5,4,3,1,2,0:T(8,128)(2,1)}) fusion(bf16[1,11,4,4,128,128]{5,4,3,1,2,0:T(8,128)(2,1)} %bitcast.6), kind=kLoop, calls=%fused_computation.82 | loop fusion | bytes 33554432 | tf_op jit(solution)/shard_map/slice | solution.py:40
  155.6 6.5 copy.8
  162.0 6.6 copy.10
  168.6 6.8 %fusion.27 = f32[8,16,128,128]{3,2,0,1:T(8,128)} fusion(bf16[8,16,128,128]{2,3,1,0:T(8,128)(2,1)} %bitcast.105, bf16[8,4,128,128]{3,2,0,1:T(8,128)(2,1)S(1)} %copy-done.7), kind=kOutput, calls=%fused_computation.39 | convolution fusion | flops 536870912 | bytes 12845056 | tf_op jit(solution)/shard_map/iab,ivbc->ivac/dot_general | solution.py:37
  179.9 6.5 copy.12
  186.4 6.7 %fusion.33 = f32[8,16,128,128]{3,2,0,1:T(8,128)} fusion(bf16[8,16,128,128]{2,3,1,0:T(8,128)(2,1)} %bitcast.108, bf16[8,4,128,128]{3,2,0,1:T(8,128)(2,1)S(1)} %copy-done.7), kind=kOutput, calls=%fused_computation.41 | convolution fusion | flops 536870912 | bytes 12845056 | tf_op jit(solution)/shard_map/iab,ivbc->ivac/dot_general | solution.py:37
  193.1 6.5 copy.14
  204.2 7.8 %pad_add_fusion.2 = bf16[8,19,128,128]{3,2,0,1:T(8,128)(2,1)S(1)} fusion(f32[8,16,128,128]{3,2,0,1:T(8,128)S(1)} %fusion.36, f32[8,16,128,128]{3,2,0,1:T(8,128)S(1)} %copy-done.1, f32[8,16,128,128]{3,2,0,1:T(8,128)} %fusion.30, f32[8,16,128,128]{3,2,0,1:T(8,128)} %fusion.27), kind=kLoop, calls=%fused_computation.8 | loop fusion | flops 9961472 | bytes 38535168 | tf_op jit(solution)/shard_map/add | solution.py:43
  221.4 37.7 %reduce-scatter.4.cloned.1.call-done = bf16[8,4,128,128]{3,2,0,1:T(8,128)(2,1)} async-done(((bf16[8,16,128,128]{3,2,0,1:T(8,128)(2,1)}), bf16[8,4,128,128]{3,2,0,1:T(8,128)(2,1)}) %reduce-scatter.4.cloned.1.call-update) | async-done | bytes 1048592 | tf_op jit(solution)/shard_map/reduce_scatter | solution.py:49
  276.1 33.3 %collective-permute-done.4 = bf16[8,4,128,128]{3,2,0,1:T(8,128)(2,1)} collective-permute-done((bf16[8,4,128,128]{3,2,0,1:T(8,128)(2,1)}, bf16[8,4,128,128]{3,2,0,1:T(8,128)(2,1)}, u32[]{:S(2)}, u32[]{:S(2)}) %collective-permute-start.4) | collective-permute-done | bytes 1048608 | tf_op jit(solution)/shard_map/ppermute | solution.py:10
  319.4 9.8 %broadcast_select_fusion = (bf16[4,11,4,128,128]{4,3,2,1,0:T(8,128)(2,1)}, bf16[4,11,4,128,128]{4,3,2,1,0:T(8,128)(2,1)}) fusion(bf16[4,11,4,128,128]{4,3,2,1,0:T(8,128)(2,1)} %bitcast.100, pred[4,11]{1,0:T(4,128)(4,1)S(1)} %compare_and_fusion, bf16[4,11,4,128,128]{4,3,2,1,0:T(8,128)(2,1)} %bitcast.99), kind=kLoop, calls=%fused_computation.12 | loop fusion | flops 5767168 | bytes 23068716 | tf_op jit(solution)/shard_map/jit(_take)/select_n | solution.py:30
  329.2 68.3 %all_to_all.45 = bf16[4,11,4,128,128]{4,3,2,1,0:T(8,128)(2,1)S(1)} all-to-all(bf16[4,11,4,128,128]{4,3,2,1,0:T(8,128)(2,1)} %get-tuple-element.20), channel_id=1, replica_groups=mesh['layer'=8,'rep'=4] {'rep'}, dimensions={0} | all-to-all | bytes 11534336 | tf_op jit(solution)/shard_map/all_to_all | solution.py:31
  397.6 6.7 fusion.65
  404.3 6.5 copy.6
  410.7 6.7 %fusion.39 = f32[8,16,128,128]{3,2,0,1:T(8,128)} fusion(bf16[8,16,128,128]{2,3,1,0:T(8,128)(2,1)} %bitcast.110, bf16[8,4,128,128]{3,2,0,1:T(8,128)(2,1)} %select_convert_fusion.2), kind=kOutput, calls=%fused_computation.43 | convolution fusion | flops 536870912 | bytes 12845056 | tf_op jit(solution)/shard_map/iab,ivbc->ivac/dot_general | solution.py:37
  417.4 6.4 copy.17
  423.9 6.7 fusion.42
  430.6 6.4 copy.19
  437.0 6.7 %fusion.45 = f32[8,16,128,128]{3,2,0,1:T(8,128)} fusion(bf16[8,16,128,128]{2,3,1,0:T(8,128)(2,1)} %bitcast.112, bf16[8,4,128,128]{3,2,0,1:T(8,128)(2,1)} %select_convert_fusion.2), kind=kOutput, calls=%fused_computation.45 | convolution fusion | flops 536870912 | bytes 12845056 | tf_op jit(solution)/shard_map/iab,ivbc->ivac/dot_general | solution.py:37
  443.7 6.4 copy.21
  454.9 7.8 %pad_add_fusion.1 = bf16[8,19,128,128]{3,2,0,1:T(8,128)(2,1)S(1)} fusion(f32[8,16,128,128]{3,2,0,1:T(8,128)S(1)} %fusion.48, f32[8,16,128,128]{3,2,0,1:T(8,128)S(1)} %copy-done, f32[8,16,128,128]{3,2,0,1:T(8,128)} %fusion.42, f32[8,16,128,128]{3,2,0,1:T(8,128)} %fusion.39), kind=kLoop, calls=%fused_computation.7 | loop fusion | flops 9961472 | bytes 38535168 | tf_op jit(solution)/shard_map/add | solution.py:43
  465.8 91.6 %all_to_all.46 = bf16[4,11,4,128,128]{4,3,2,1,0:T(8,128)(2,1)S(1)} all-to-all(bf16[4,11,4,128,128]{4,3,2,1,0:T(8,128)(2,1)} %get-tuple-element.19), channel_id=1, replica_groups=mesh['layer'=8,'rep'=4] {'rep'}, dimensions={0} | all-to-all | bytes 11534336 | tf_op jit(solution)/shard_map/all_to_all | solution.py:31
  557.4 6.7 %fusion.64 = (bf16[1,8,4,4,128,128]{5,4,3,1,2,0:T(8,128)(2,1)}, bf16[1,8,4,4,128,128]{5,4,3,1,2,0:T(8,128)(2,1)}, bf16[1,8,4,4,128,128]{5,4,3,1,2,0:T(8,128)(2,1)}, bf16[1,8,4,4,128,128]{5,4,3,1,2,0:T(8,128)(2,1)}) fusion(bf16[1,11,4,4,128,128]{5,4,3,1,2,0:T(8,128)(2,1)S(1)} %bitcast.97), kind=kLoop, calls=%fused_computation.80 | loop fusion | bytes 33554432 | tf_op jit(solution)/shard_map/slice | solution.py:40
  564.1 6.5 copy.23
  570.7 6.4 copy.25
  577.1 6.5 copy.27
  583.6 6.5 copy.29
  597.2 6.7 %fusion.60 = f32[8,16,128,128]{3,2,0,1:T(8,128)} fusion(bf16[8,16,128,128]{2,3,1,0:T(8,128)(2,1)} %bitcast.104, bf16[8,4,128,128]{3,2,0,1:T(8,128)(2,1)S(1)} %copy-done.6), kind=kOutput, calls=%fused_computation.50 | convolution fusion | flops 536870912 | bytes 12845056 | tf_op jit(solution)/shard_map/iab,ivbc->ivac/dot_general | solution.py:37
  603.9 6.0 pad_add_fusion
  613.0 44.0 %reduce-scatter.8.cloned.1.call-done = bf16[8,4,128,128]{3,2,0,1:T(8,128)(2,1)} async-done(((bf16[8,16,128,128]{3,2,0,1:T(8,128)(2,1)}), bf16[8,4,128,128]{3,2,0,1:T(8,128)(2,1)}) %reduce-scatter.8.cloned.1.call-update) | async-done | bytes 1048592 | tf_op jit(solution)/shard_map/reduce_scatter | solution.py:49
  (68 shorter events, 98.9 us)
Async XLA Ops:
  10.6 47.4 %copy-start.5 = (bf16[8,4,128,128]{3,2,0,1:T(8,128)(2,1)}, bf16[8,4,128,128]{3,2,0,1:T(8,128)(2,1)S(1)}, u32[]{:S(2)}) copy-start(bf16[8,4,128,128]{3,2,0,1:T(8,128)(2,1)S(1)} %get-tuple-element.21) | copy-start | bytes 3145732
  10.6 47.4 %collective-permute-start.2 = (bf16[8,4,128,128]{3,2,0,1:T(8,128)(2,1)S(1)}, bf16[8,4,128,128]{3,2,0,1:T(8,128)(2,1)S(1)}, u32[]{:S(2)}, u32[]{:S(2)}) collective-permute-start(bf16[8,4,128,128]{3,2,0,1:T(8,128)(2,1)S(1)} %get-tuple-element.21), channel_id=1, source_target_pairs={{0,4},{4,8},{8,12},{12,16},{16,20},{20,24},{24,28},{1,5},{5,9},{9,... | collective-permute-start | bytes 3145736 | tf_op jit(solution)/shard_map/ppermute | solution.py:10
  13.7 47.3 %collective-permute-start.3 = (bf16[8,4,128,128]{3,2,0,1:T(8,128)(2,1)S(1)}, bf16[8,4,128,128]{3,2,0,1:T(8,128)(2,1)}, u32[]{:S(2)}, u32[]{:S(2)}) collective-permute-start(bf16[8,4,128,128]{3,2,0,1:T(8,128)(2,1)S(1)} %get-tuple-element.21), channel_id=1, source_target_pairs={{4,0},{8,4},{12,8},{16,12},{20,16},{24,20},{28,24},{5,1},{9,5},{13... | collective-permute-start | bytes 3145736 | tf_op jit(solution)/shard_map/ppermute | solution.py:10
  58.0 1.0 copy-start.9
  73.6 69.7 %all-to-all-start.1 = ((bf16[4,11,4,128,128]{4,3,2,1,0:T(8,128)(2,1)}), bf16[4,11,4,128,128]{4,3,2,1,0:T(8,128)(2,1)}, u32[]{:S(2)}, u32[]{:S(2)}) async-start(bf16[4,11,4,128,128]{4,3,2,1,0:T(8,128)(2,1)} %broadcast_select_fusion.1), calls=%async_computation.1 | async-start | bytes 11534336 | tf_op jit(solution)/shard_map/all_to_all | solution.py:31
  79.2 179.9 %reduce-scatter.4.cloned.1.call-start = ((), (), s32[]{:S(2)}) async-start(), calls=%async_computation.6 | async-start | bytes 5242880 | tf_op jit(solution)/shard_map/reduce_scatter | solution.py:49
  162.0 6.6 copy-start.7
  168.6 6.8 %copy-start.4 = (bf16[1,8,4,4,128,128]{4,5,3,2,1,0:T(8,128)(2,1)S(1)}, bf16[1,8,4,4,128,128]{4,5,3,2,1,0:T(8,128)(2,1)}, u32[]{:S(2)}) copy-start(bf16[1,8,4,4,128,128]{4,5,3,2,1,0:T(8,128)(2,1)} %copy.10) | copy-start | bytes 12582916
  199.5 4.6 copy-start.1
  215.0 397.9 %reduce-scatter.6.cloned.1.call-start = ((), (), s32[]{:S(2)}) async-start(), calls=%async_computation.7 | async-start | bytes 5242880 | tf_op jit(solution)/shard_map/reduce_scatter | solution.py:49
  215.1 53.2 %collective-permute-start = (bf16[8,4,128,128]{3,2,0,1:T(8,128)(2,1)S(1)}, bf16[8,4,128,128]{3,2,0,1:T(8,128)(2,1)S(1)}, u32[]{:S(2)}, u32[]{:S(2)}) collective-permute-start(bf16[8,4,128,128]{3,2,0,1:T(8,128)(2,1)S(1)} %copy-done.7), channel_id=1, source_target_pairs={{0,4},{4,8},{8,12},{12,16},{16,20},{20,24},{24,28},{1,5},{5,9},{9,... | collective-permute-start | bytes 3145736 | tf_op jit(solution)/shard_map/ppermute | solution.py:10
  218.2 51.1 %collective-permute-start.1 = (bf16[8,4,128,128]{3,2,0,1:T(8,128)(2,1)S(1)}, bf16[8,4,128,128]{3,2,0,1:T(8,128)(2,1)}, u32[]{:S(2)}, u32[]{:S(2)}) collective-permute-start(bf16[8,4,128,128]{3,2,0,1:T(8,128)(2,1)S(1)} %copy-done.7), channel_id=1, source_target_pairs={{4,0},{8,4},{12,8},{16,12},{20,16},{24,20},{28,24},{5,1},{9,5},{13... | collective-permute-start | bytes 3145736 | tf_op jit(solution)/shard_map/ppermute | solution.py:10
  261.9 47.5 %collective-permute-start.4 = (bf16[8,4,128,128]{3,2,0,1:T(8,128)(2,1)}, bf16[8,4,128,128]{3,2,0,1:T(8,128)(2,1)}, u32[]{:S(2)}, u32[]{:S(2)}) collective-permute-start(bf16[8,4,128,128]{3,2,0,1:T(8,128)(2,1)} %select_convert_fusion.2), channel_id=1, source_target_pairs={{0,4},{4,8},{8,12},{12,16},{16,20},{20,24},{24,28},{1,5},{5,9},{9,... | collective-permute-start | bytes 3145736 | tf_op jit(solution)/shard_map/ppermute | solution.py:10
  265.0 47.6 %collective-permute-start.5 = (bf16[8,4,128,128]{3,2,0,1:T(8,128)(2,1)}, bf16[8,4,128,128]{3,2,0,1:T(8,128)(2,1)}, u32[]{:S(2)}, u32[]{:S(2)}) collective-permute-start(bf16[8,4,128,128]{3,2,0,1:T(8,128)(2,1)} %select_convert_fusion.2), channel_id=1, source_target_pairs={{4,0},{8,4},{12,8},{16,12},{20,16},{24,20},{28,24},{5,1},{9,5},{13... | collective-permute-start | bytes 3145736 | tf_op jit(solution)/shard_map/ppermute | solution.py:10
  268.3 1.0 copy-start.8
  450.2 4.7 copy-start
  465.8 191.2 %reduce-scatter.8.cloned.1.call-start = ((), (), s32[]{:S(2)}) async-start(), calls=%async_computation.8 | async-start | bytes 5242880 | tf_op jit(solution)/shard_map/reduce_scatter | solution.py:49
  583.6 6.5 copy-start.6
  590.1 3.6 copy-start.2
  593.8 2.2 copy-start.3
Sparse Core Ops, SparseCore 0:
  215.2 43.8 reduce-scatter.3
  465.9 66.6 reduce-scatter.5
  613.1 43.8 reduce-scatter.7
where the time goes:
time: 675 us; the launch traced here: 668 us
  waiting for transfers between devices  225 us (33%)
  blocking collectives  160 us (24%)
  local copies, waits for them, and re-layouts  134 us (20%)
  matrix products  58.1 us (9%)
  other arithmetic  51.9 us (8%)
  starting transfers between devices  24.6 us (4%)
  between operations  14.4 us (2%)
    all_to_all x2, blocking collectives, band_product(): lax.all_to_all(outgoing, 'rep', split_axis=0, concat_axis=2, tiled=True)[0]  160 us
    slice x15, local copies, waits for them, and re-layouts, band_product(): incoming[local_slot:local_slot + row_count]  103 us
    reduce_scatter x3, waiting for transfers between devices, band_product(): lax.psum_scatter(partial_value.astype(jnp.bfloat16), 'rep', scatter_dimen...  81.7 us
    ppermute x6, waiting for transfers between devices, passed_along(): return lax.ppermute(block, axis, route)  79.4 us
    all_to_all x1, waiting for transfers between devices, band_product(): lax.all_to_all(outgoing, 'rep', split_axis=0, concat_axis=2, tiled=True)[0]  63.9 us
    dot_general x12, matrix products, band_product(): jnp.einsum('iab,ivbc->ivac', left_tiles[:, local_slot], incoming[local_sl...  58.1 us
    add x3, other arithmetic, band_product(): summed + jnp.pad(product, ((0, 0), (local_slot, slot_count - 1 - local_sl...  21.5 us
    ppermute x6, starting transfers between devices, passed_along(): return lax.ppermute(block, axis, route)  18.7 us
  transfers between devices with their start and end apart: 10, of which 7 were waited for; matrix products, arithmetic and copies ran while one was open for 10% of the time, Pallas kernels for 0%

commit v1 on v0

v1 whole, which is shorter than its diff:
```python
import functools

import jax
import jax.numpy as jnp
from jax import lax
from jax.experimental import pallas as pl
from jax.experimental.pallas import tpu as pltpu
from jax.sharding import PartitionSpec as P

MESH = pl.DeviceIdType.MESH
ANY = pl.BlockSpec(memory_space=pl.ANY)
VMEM = pl.BlockSpec(memory_space=pltpu.VMEM)
SMEM = pl.BlockSpec(memory_space=pltpu.SMEM)


def reached(rows, band, low, high):
    half = band // 2
    found = {1: {}, -1: {}}
    for i in range(rows):
        for u in range(band):
            j = i - half + u
            if 0 <= j < rows:
                continue
            assert -rows <= j < 2 * rows
            side, a = (1, j + rows) if j < 0 else (-1, j - rows)
            for w in range(low, high):
                v = w + half - u
                if 0 <= v < band:
                    lo, hi = found[side].get(a, (v, v + 1))
                    found[side][a] = (min(lo, v), max(hi, v + 1))
    return found


def rectangles(spans, first, last):
    cut = []
    for a in sorted(spans):
        lo, hi = max(spans[a][0], first), min(spans[a][1], last)
        if lo >= hi:
            continue
        if cut and cut[-1][1] == a and cut[-1][2:] == (lo, hi):
            cut[-1] = (cut[-1][0], a + 1, lo, hi)
        else:
            cut.append((a, a + 1, lo, hi))
    return cut


def exchange_kernel(layers, reps, rows, slots, streams, *refs):
    count = len(streams)
    sources = refs[:count]
    outs = list(refs[count : len(refs) - 3])
    send_sems, recv_sems, local_sems = refs[-3:]
    band = slots * reps
    layer = lax.axis_index("layer")
    rep = lax.axis_index("rep")
    bits = []
    bit = reps // 2
    while bit >= 2:
        bits.append(bit)
        bit //= 2
    masks = list(range(0, reps, 2))
    keys = {}

    barrier = pltpu.get_barrier_semaphore()
    after, before = lax.rem(layer + 1, layers), lax.rem(layer + layers - 1, layers)
    for place in (after, before):
        pl.semaphore_signal(barrier, inc=1, device_id={"layer": place}, device_id_type=MESH)
    for flip in [1] + bits:
        partner = rep + flip * (1 - 2 * lax.rem(lax.div(rep, flip), 2))
        pl.semaphore_signal(barrier, inc=1, device_id={"rep": partner}, device_id_type=MESH)
    pl.semaphore_wait(barrier, 3 + len(bits))

    def number(key):
        return keys.setdefault(key, len(keys))

    def schedule(me):
        chip = me // 2
        spans = reached(rows, band, chip * 2 * slots, (chip + 1) * 2 * slots)
        remote = []

        def own(s):
            gather, halo = streams[s]
            if not gather:
                return sources[s]
            return outs[s].at[pl.ds(rows, rows)] if halo else outs[s]

        def shard(ref, q):
            return ref.at[:, pl.ds(q * slots, slots)]

        def copy(key, src, dst, device):
            n = number(key)
            return pltpu.make_async_remote_copy(
                src_ref=src, dst_ref=dst, send_sem=send_sems.at[n], recv_sem=recv_sems.at[n],
                device_id=device, device_id_type=MESH,
            )

        def begin(guard, made):
            remote.append((guard, made))
            if guard is None:
                made.start()
            else:
                @pl.when(guard)
                def _():
                    made.start()

        def across(s, m, bit):
            q = me ^ bit ^ m
            src = sources[s] if q == me else shard(own(s), q)
            return copy(("y", s, m), src, shard(own(s), q), {"rep": me ^ bit})

        def to_core(s, m):
            q = me ^ m
            src = sources[s] if m == 0 else shard(own(s), q)
            return copy(("d", s, m), src, shard(own(s), q), {"rep": me ^ 1})

        def halo_base(side):
            return 0 if side == 1 else 2 * rows

        def to_layer(s, side, m, k, piece):
            q = me ^ m
            a, b, lo, hi = piece
            if m == 0 and streams[s][0]:
                src = sources[s].at[pl.ds(a, b - a), pl.ds(lo - q * slots, hi - lo)]
            else:
                src = own(s).at[pl.ds(a, b - a), pl.ds(lo, hi - lo)]
            dst = outs[s].at[pl.ds(halo_base(side) + a, b - a), pl.ds(lo, hi - lo)]
            return copy(("x", s, side, m, k), src, dst, {"layer": after if side == 1 else before})

        def halo_to_core(s, side, m, q):
            cut = rectangles(spans[side], q * slots, (q + 1) * slots)
            a, b = min(c[0] for c in cut), max(c[1] for c in cut)
            part = outs[s].at[pl.ds(halo_base(side) + a, b - a), pl.ds(q * slots, slots)]
            return copy(("h", s, side, m), part, part, {"rep": me ^ 1})

        may_send = {1: layer + 1 < layers, -1: layer > 0}
        may_take = {1: layer > 0, -1: layer + 1 < layers}

        def pieces(side, m):
            q = me ^ m
            return rectangles(spans[side], q * slots, (q + 1) * slots)

        def send_layer(s, m):
            for side in (1, -1):
                for k, piece in enumerate(pieces(side, m)):
                    begin(may_send[side], to_layer(s, side, m, k, piece))

        gathered = [s for s in range(count) if streams[s][0]]
        haloed = [s for s in range(count) if streams[s][1]]
        locals_ = []
        for s in gathered:
            if bits:
                begin(None, across(s, bits[0], bits[0]))
            begin(None, to_core(s, 0))
            kept = pltpu.make_async_copy(sources[s], shard(own(s), me), local_sems.at[s])
            kept.start()
            locals_.append(kept)
        for s in haloed:
            send_layer(s, 0)
        for s in haloed:
            if not streams[s][0]:
                for m in masks[1:]:
                    send_layer(s, m)
        for s in gathered:
            held = [0]
            for n, bit in enumerate(bits):
                if n > 0:
                    for m in held:
                        begin(None, across(s, m ^ bit, bit))
                fresh = [m ^ bit for m in held]
                for m in fresh:
                    across(s, m, bit).wait_recv()
                    begin(None, to_core(s, m))
                    if streams[s][1]:
                        send_layer(s, m)
                held = held + fresh
        for m in masks:
            for s in haloed:
                for side in (1, -1):
                    cut = pieces(side, m)
                    if not cut:
                        continue
                    onward = halo_to_core(s, side, m, me ^ m)
                    remote.append((may_take[side], onward))

                    @pl.when(may_take[side])
                    def _(s=s, side=side, m=m, cut=cut, onward=onward):
                        for k, piece in enumerate(cut):
                            to_layer(s, side, m, k, piece).wait_recv()
                        onward.start()
        for s in gathered:
            for m in masks:
                copy(("d", s, m), sources[s], shard(own(s), me ^ 1 ^ m), {"rep": me ^ 1}).wait_recv()
        for s in haloed:
            for side in (1, -1):
                for m in masks:
                    if not rectangles(spans[side], (me ^ 1 ^ m) * slots, ((me ^ 1 ^ m) + 1) * slots):
                        continue

                    @pl.when(may_take[side])
                    def _(s=s, side=side, m=m):
                        halo_to_core(s, side, m, me ^ 1 ^ m).wait_recv()
        for kept in locals_:
            kept.wait()
        for guard, made in remote:
            if guard is None:
                made.wait_send()
            else:
                @pl.when(guard)
                def _(made=made):
                    made.wait_send()

    for me in range(reps):
        pl.when(rep == me)(functools.partial(schedule, me))
    assert len(keys) <= send_sems.shape[0]


def exchange(layers, reps, rows, slots, streams, arrays, call_id):
    tile = arrays[0].shape[2:]
    band = slots * reps
    shapes = [
        jax.ShapeDtypeStruct(((3 * rows if halo else rows), band) + tile, jnp.bfloat16) for _, halo in streams
    ]
    sems = 128
    return pl.pallas_call(
        functools.partial(exchange_kernel, layers, reps, rows, slots, streams),
        out_shape=shapes,
        in_specs=[VMEM if gather else ANY for gather, _ in streams],
        out_specs=[ANY] * len(streams),
        scratch_shapes=[
            pltpu.SemaphoreType.DMA((sems,)),
            pltpu.SemaphoreType.DMA((sems,)),
            pltpu.SemaphoreType.DMA((len(streams),)),
        ],
        compiler_params=pltpu.CompilerParams(collective_id=call_id, has_side_effects=True),
        name=f"exchange{call_id}",
    )(*arrays)


def product_row(i, left, right, layer, rep, layers, rows, slots, band):
    half = band // 2
    step = 4
    total = None
    for first in range(0, band, step):
        wide = jnp.concatenate([left(i, u) for u in range(first, first + step)], axis=1)
        tall = []
        for u in range(first, first + step):
            row = layer * rows + i - half + u
            inside = jnp.logical_and(row >= 0, row < layers * rows)
            tiles = []
            for w in range(slots):
                v = rep * slots + w + half - u
                good = jnp.logical_and(inside, jnp.logical_and(v >= 0, v < band))
                part = right[i + u + rows - half, jnp.clip(v, 0, band - 1)]
                tiles.append(jnp.where(good, part, jnp.zeros_like(part)))
            tall.append(jnp.concatenate(tiles, axis=1))
        piece = jnp.dot(wide, jnp.concatenate(tall, axis=0), preferred_element_type=jnp.float32)
        total = piece if total is None else total + piece
    return total


def update_kernel(layers, pattern, z_full, y_wide, out):
    rows, slots, tile = out.shape[0], out.shape[1], out.shape[2]
    band = z_full.shape[1]
    layer, rep = lax.axis_index("layer"), lax.axis_index("rep")
    across = lax.broadcasted_iota(jnp.int32, (tile, tile), 0)
    down = lax.broadcasted_iota(jnp.int32, (tile, tile), 1)
    identity = jnp.where(across == down, 1.5, 0.0).astype(jnp.float32)

    def step(i, _):
        total = product_row(i, lambda i, u: z_full[i, u], y_wide, layer, rep, layers, rows, slots, band)
        for w in range(slots):
            value = -0.5 * total[:, w * tile : (w + 1) * tile]
            value = value + jnp.where(rep * slots + w == band // 2, identity, 0.0)
            out[i, w] = jnp.where(pattern[i, w] == 1, value, 0.0).astype(out.dtype)
        return 0

    lax.fori_loop(0, rows, step, 0)


def final_kernel(layers, pattern, y_wide, u_wide, z_full, z_halo, z_next, y_next, y_own, u_all, z_all, sems):
    rows, slots, tile = z_next.shape[0], z_next.shape[1], z_next.shape[2]
    band = z_full.shape[1]
    layer, rep = lax.axis_index("layer"), lax.axis_index("rep")
    low, mid, high = pl.ds(0, rows), pl.ds(rows, rows), pl.ds(2 * rows, rows)
    copies = [
        pltpu.make_async_copy(y_wide.at[mid], y_own, sems.at[0]),
        pltpu.make_async_copy(u_wide, u_all, sems.at[1]),
        pltpu.make_async_copy(z_halo.at[low], z_all.at[low], sems.at[2]),
        pltpu.make_async_copy(z_full, z_all.at[mid], sems.at[3]),
        pltpu.make_async_copy(z_halo.at[high], z_all.at[high], sems.at[4]),
    ]
    for made in copies:
        made.start()
    for made in copies:
        made.wait()

    def step(i, _):
        jobs = (
            (lambda i, u: y_own[i, u], u_all, y_next),
            (lambda i, u: u_all[i + rows, u], z_all, z_next),
        )
        for left, right, out in jobs:
            total = product_row(i, left, right, layer, rep, layers, rows, slots, band)
            for w in range(slots):
                value = total[:, w * tile : (w + 1) * tile]
                out[i, w] = jnp.where(pattern[i, w] == 1, value, 0.0).astype(out.dtype)
        return 0

    lax.fori_loop(0, rows, step, 0)


def solution(mesh):
    layers, reps = mesh.shape["layer"], mesh.shape["rep"]

    def body(inverse_root, square_root, pattern):
        rows, slots = pattern.shape
        tile = inverse_root.shape[2:]
        band = slots * reps
        in_pattern = (pattern == 1)[:, :, None, None]
        z = jnp.where(in_pattern, inverse_root, jnp.zeros_like(inverse_root))
        y = jnp.where(in_pattern, square_root, jnp.zeros_like(square_root))
        limit = pltpu.CompilerParams(vmem_limit_bytes=56 * 1024 * 1024)
        local = jax.ShapeDtypeStruct((rows, slots) + tile, jnp.bfloat16)
        y_wide, z_full = exchange(layers, reps, rows, slots, ((True, True), (True, False)), (y, z), 0)
        u = pl.pallas_call(
            functools.partial(update_kernel, layers),
            out_shape=local,
            in_specs=[SMEM, VMEM, VMEM],
            out_specs=VMEM,
            compiler_params=limit,
            name="update",
        )(pattern, z_full, y_wide)
        u_wide, z_halo = exchange(layers, reps, rows, slots, ((True, True), (False, True)), (u, z_full), 1)
        z_next, y_next = pl.pallas_call(
            functools.partial(final_kernel, layers),
            out_shape=[local, local],
            in_specs=[SMEM, ANY, ANY, ANY, ANY],
            out_specs=[VMEM, VMEM],
            scratch_shapes=[
                pltpu.VMEM((rows, band) + tile, jnp.bfloat16),
                pltpu.VMEM((3 * rows, band) + tile, jnp.bfloat16),
                pltpu.VMEM((3 * rows, band) + tile, jnp.bfloat16),
                pltpu.SemaphoreType.DMA((5,)),
            ],
            compiler_params=limit,
            name="final",
        )(pattern, y_wide, u_wide, z_full, z_halo)
        return z_next, y_next

    placed = P("layer", "rep", None, None)
    return jax.shard_map(
        body,
        mesh=mesh,
        in_specs=(placed, placed, P("layer", "rep")),
        out_specs=(placed, placed),
        check_vma=False,
    )
```

time: 675 us -> 193 us (0.29)
  waiting for transfers between devices: 225 us -> 0 us
  Pallas kernels: 0 us -> 187 us
  blocking collectives: 160 us -> 0 us
  local copies, waits for them, and re-layouts: 134 us -> 1.44 us
  matrix products: 58.1 us -> 0 us
  other arithmetic: 51.9 us -> 3.75 us
  starting transfers between devices: 24.6 us -> 0 us
  between operations: 14.4 us -> 0.65 us
    pallas_call x0 -> x4, Pallas kernels: none -> 187 us  [the longest x2 156 us: exchange(): pl.pallas_call(functools.partial(exchange_kernel, layers, reps, rows, slo...]
    all_to_all x2 -> x0, blocking collectives: 160 us -> none  [band_product(): lax.all_to_all(outgoing, 'rep', split_axis=0, concat_axis=2, tiled=True)[0]]
    slice x15 -> x0, local copies, waits for them, and re-layouts: 103 us -> none  [band_product(): incoming[local_slot:local_slot + row_count]]
    reduce_scatter x3 -> x0, waiting for transfers between devices: 81.7 us -> none  [band_product(): lax.psum_scatter(partial_value.astype(jnp.bfloat16), 'rep', scatter_dimen...]
    ppermute x6 -> x0, waiting for transfers between devices: 79.4 us -> none  [passed_along(): return lax.ppermute(block, axis, route)]
    all_to_all x1 -> x0, waiting for transfers between devices: 63.9 us -> none  [band_product(): lax.all_to_all(outgoing, 'rep', split_axis=0, concat_axis=2, tiled=True)[0]]
    dot_general x12 -> x0, matrix products: 58.1 us -> none  [band_product(): jnp.einsum('iab,ivbc->ivac', left_tiles[:, local_slot], incoming[local_sl...]
    add x3 -> x0, other arithmetic: 21.5 us -> none  [band_product(): summed + jnp.pad(product, ((0, 0), (local_slot, slot_count - 1 - local_sl...]
  transfers between devices with their start and end apart: 10 -> 0, of which waited for: 7 -> 0; matrix products, arithmetic and copies ran while one was open for 10% -> 0% of each run, Pallas kernels for 0% -> 0%
where the time goes in v1:
time: 193 us
  Pallas kernels  187 us (97%)
  other arithmetic  3.75 us (2%)
    pallas_call x2, Pallas kernels, exchange(): pl.pallas_call(functools.partial(exchange_kernel, layers, reps, rows, slo...  156 us
    pallas_call x1, Pallas kernels, body(): pl.pallas_call(functools.partial(final_kernel, layers), out_shape=[local,...  19.8 us
    pallas_call x1, Pallas kernels, body(): pl.pallas_call(functools.partial(update_kernel, layers), out_shape=local,...  11.1 us

profile of v1, /device:TPU:17, one launch (start us, length us, event | category | flops | bytes accessed | tf_op | source)
XLA Modules:
  0.0 193.0 jit_solution(18024824536310054482)
XLA Ops:
  0.6 0.7 broadcast_compare_fusion
  1.3 0.1 copy.5
  1.4 1.3 copy.7.pattern
  2.8 3.1 %broadcast_select_fusion = (bf16[8,4,128,128]{3,2,1,0:T(8,128)(2,1)}, bf16[8,4,128,128]{3,2,1,0:T(8,128)(2,1)}) fusion(bf16[8,4,128,128]{3,2,1,0:T(8,128)(2,1)} %param.3, pred[8,4]{1,0:T(8,128)(4,1)S(1)} %copy.5, bf16[8,4,128,128]{3,2,1,0:T(8,128)(2,1)} %param.4), kind=kLoop, calls=%fused_computation | loop fusion | flops 1048576 | bytes 4194336 | tf_op jit(solution)/shard_map/jit(_where)/select_n | solution.py:319
  5.8 58.9 %exchange0.1 = (bf16[24,16,128,128]{3,2,1,0:T(8,128)(2,1)}, bf16[8,16,128,128]{3,2,1,0:T(8,128)(2,1)}) custom-call(bf16[8,4,128,128]{3,2,1,0:T(8,128)(2,1)} %get-tuple-element.11.refs_0_, bf16[8,4,128,128]{3,2,1,0:T(8,128)(2,1)} %get-tuple-element.10.refs_1_), custom_call_target="tpu_custom_call" | custom-call | tf_op jit(solution)/shard_map/exchange0/pallas_call | solution.py:223
  64.7 11.1 %update.1.refs_0_ = bf16[8,4,128,128]{3,2,1,0:T(8,128)(2,1)} custom-call(s32[8,4]{1,0:T(8,128)} %copy.7.pattern, bf16[8,16,128,128]{3,2,1,0:T(8,128)(2,1)} %get-tuple-element.7.z_full.refs_1_, bf16[24,16,128,128]{3,2,1,0:T(8,128)(2,1)} %get-tuple-element.6.y_wide), custom_call_target="tpu_custom_call" | custom-call | tf_op jit(solution)/shard_map/update/pallas_call | solution.py:324
  75.9 97.3 %exchange1.1 = (bf16[24,16,128,128]{3,2,1,0:T(8,128)(2,1)}, bf16[24,16,128,128]{3,2,1,0:T(8,128)(2,1)}) custom-call(bf16[8,4,128,128]{3,2,1,0:T(8,128)(2,1)} %update.1.refs_0_, bf16[8,16,128,128]{3,2,1,0:T(8,128)(2,1)} %get-tuple-element.7.z_full.refs_1_), custom_call_target="tpu_custom_call" | custom-call | tf_op jit(solution)/shard_map/exchange1/pallas_call | solution.py:223
  173.1 19.8 %final.1 = (bf16[8,4,128,128]{3,2,1,0:T(8,128)(2,1)}, bf16[8,4,128,128]{3,2,1,0:T(8,128)(2,1)}) custom-call(s32[8,4]{1,0:T(8,128)} %copy.7.pattern, bf16[24,16,128,128]{3,2,1,0:T(8,128)(2,1)} %get-tuple-element.6.y_wide, bf16[24,16,128,128]{3,2,1,0:T(8,128)(2,1)} %get-tuple-element.8.u_wide, bf16[8,16,128,128]{3,2,1,0:T(8,128)(2,1)} %get-tuple-element.7.z_full.refs_1_, ...), custom_call_target="tpu_custom_call" | custom-call | tf_op jit(solution)/shard_map/final/pallas_call | solution.py:333

commit v2 on v1

v2 whole, which is shorter than its diff:
```python
import functools

import jax
import jax.numpy as jnp
from jax import lax
from jax.experimental import pallas as pl
from jax.experimental.pallas import tpu as pltpu
from jax.sharding import PartitionSpec as P

MESH = pl.DeviceIdType.MESH
VMEM = pl.BlockSpec(memory_space=pltpu.VMEM)
SMEM = pl.BlockSpec(memory_space=pltpu.SMEM)
SEMAPHORES = 256


def reached(rows, band, low, high):
    half = band // 2
    found = {1: {}, -1: {}}
    for i in range(rows):
        for u in range(band):
            j = i - half + u
            if 0 <= j < rows:
                continue
            assert -rows <= j < 2 * rows
            side, a = (1, j + rows) if j < 0 else (-1, j - rows)
            for w in range(low, high):
                v = w + half - u
                if 0 <= v < band:
                    lo, hi = found[side].get(a, (v, v + 1))
                    found[side][a] = (min(lo, v), max(hi, v + 1))
    return found


def rectangles(spans, first, last):
    cut = []
    for a in sorted(spans):
        lo, hi = max(spans[a][0], first), min(spans[a][1], last)
        if lo >= hi:
            continue
        if cut and cut[-1][1] == a and cut[-1][2:] == (lo, hi):
            cut[-1] = (cut[-1][0], a + 1, lo, hi)
        else:
            cut.append((a, a + 1, lo, hi))
    return cut


class Later:
    def __init__(self, make, args=None):
        self.make, self.args = make, args

    def __call__(self, *args):
        return Later(self.make, args)

    def start(self):
        self.make(*self.args).start()

    def wait_recv(self):
        self.make(*self.args).wait_recv()

    def wait_send(self):
        self.make(*self.args).wait_send()


def step_kernel(layers, reps, refs_shape, pattern, z_own, y_own, z_next, y_next, y_wide, z_wide, u_wide, send_sems, recv_sems):
    rows, slots, tile = refs_shape
    band = slots * reps
    half = band // 2
    layer, rep = lax.axis_index("layer"), lax.axis_index("rep")
    after, before = lax.rem(layer + 1, layers), lax.rem(layer + layers - 1, layers)
    may_send = {1: layer + 1 < layers, -1: layer > 0}
    may_take = {1: layer > 0, -1: layer + 1 < layers}
    bits = []
    bit = reps // 2
    while bit >= 2:
        bits.append(bit)
        bit //= 2
    masks = list(range(0, reps, 2))
    keys = {}
    wides = {"y": y_wide, "z": z_wide, "u": u_wide}
    relayed = ("z", "u") if reps == 4 else ()

    def keep(i, _):
        for w in range(slots):
            good = pattern[i, w] == 1
            for own, wide in ((y_own, y_wide), (z_own, z_wide)):
                part = own[i, w]
                wide[rows + i, rep * slots + w] = jnp.where(good, part, jnp.zeros_like(part))
        return 0

    lax.fori_loop(0, rows, keep, 0)

    barrier = pltpu.get_barrier_semaphore()
    for place in (after, before):
        pl.semaphore_signal(barrier, inc=1, device_id={"layer": place}, device_id_type=MESH)
    for flip in [1] + bits:
        partner = rep + flip * (1 - 2 * lax.rem(lax.div(rep, flip), 2))
        pl.semaphore_signal(barrier, inc=1, device_id={"rep": partner}, device_id_type=MESH)
    pl.semaphore_wait(barrier, 3 + len(bits))

    def schedule(me):
        chip = me // 2
        remote = []
        need = reached(rows, band, chip * 2 * slots, (chip + 1) * 2 * slots)
        union = reached(rows, band, 0, band)
        other = reached(rows, band, (1 - chip) * 2 * slots, (2 - chip) * 2 * slots) if relayed else None
        direct_side = 1 if chip == 0 else -1

        def spans(s, side):
            if s not in relayed:
                return need[side]
            return union[side] if side == direct_side else {}

        def arriving(s, side):
            return spans(s, side) or need[side]

        def cut(which, q):
            return rectangles(which, q * slots, (q + 1) * slots)

        def base(side):
            return 0 if side == 1 else 2 * rows

        def copy(key, src, dst, device):
            n = keys.setdefault(key, len(keys))
            return pltpu.make_async_remote_copy(
                src_ref=src, dst_ref=dst, send_sem=send_sems.at[n], recv_sem=recv_sems.at[n],
                device_id=device, device_id_type=MESH,
            )

        def begin(guard, made):
            remote.append((guard, made))
            if guard is None:
                made.start()
            else:
                pl.when(guard)(made.start)

        def shard(s, q):
            return wides[s].at[pl.ds(rows, rows), pl.ds(q * slots, slots)]

        @Later
        def across(s, m, bit):
            part = shard(s, me ^ bit ^ m)
            return copy(("y", s, m), part, part, {"rep": me ^ bit})

        @Later
        def across_in(s, m, bit):
            part = shard(s, me ^ m)
            return copy(("y", s, m), part, part, {"rep": me ^ bit})

        @Later
        def to_core(s, m):
            part = shard(s, me ^ m)
            return copy(("d", s, m), part, part, {"rep": me ^ 1})

        @Later
        def to_core_in(s, m):
            part = shard(s, me ^ 1 ^ m)
            return copy(("d", s, m), part, part, {"rep": me ^ 1})

        @Later
        def to_layer(s, side, m, k, piece):
            a, b, lo, hi = piece
            src = wides[s].at[pl.ds(rows + a, b - a), pl.ds(lo, hi - lo)]
            dst = wides[s].at[pl.ds(base(side) + a, b - a), pl.ds(lo, hi - lo)]
            return copy(("x", s, side, m, k), src, dst, {"layer": after if side == 1 else before})

        @Later
        def relay(s, side, m, k, piece):
            a, b, lo, hi = piece
            part = wides[s].at[pl.ds(base(side) + a, b - a), pl.ds(lo, hi - lo)]
            return copy(("r", s, side, m, k), part, part, {"rep": me ^ 2})

        @Later
        def halo_to_core(s, side, m, q):
            pieces = cut(arriving(s, side), q)
            a, b = min(c[0] for c in pieces), max(c[1] for c in pieces)
            part = wides[s].at[pl.ds(base(side) + a, b - a), pl.ds(q * slots, slots)]
            return copy(("h", s, side, m), part, part, {"rep": me ^ 1})

        def send_layer(s, m):
            for side in (1, -1):
                for k, piece in enumerate(cut(spans(s, side), me ^ m)):
                    begin(may_send[side], to_layer(s, side, m, k, piece))

        def take_direct(s, m):
            for side in (1, -1):
                pieces = cut(spans(s, side), me ^ m)
                if pieces:
                    made = [to_layer(s, side, m, k, piece) for k, piece in enumerate(pieces)]
                    onward = [halo_to_core(s, side, m, me ^ m)]
                    if s in relayed:
                        onward += [
                            relay(s, side, m ^ 2, k, piece)
                            for k, piece in enumerate(cut(other[side], me ^ m))
                        ]
                    pass_on(side, made, onward)

        def take_relayed(s, m):
            for side in (1, -1):
                if s in relayed and side != direct_side:
                    pieces = cut(need[side], me ^ m)
                    if pieces:
                        made = [relay(s, side, m, k, piece) for k, piece in enumerate(pieces)]
                        pass_on(side, made, [halo_to_core(s, side, m, me ^ m)])

        def pass_on(side, made, onward):
            remote.extend((may_take[side], o) for o in onward)

            @pl.when(may_take[side])
            def _():
                for one in made:
                    one.wait_recv()
                for one in onward:
                    one.start()

        def start_gather(s):
            if bits:
                begin(None, across(s, bits[0], bits[0]))
            begin(None, to_core(s, 0))

        def gather(s, halo):
            held = [0]
            for n, bit in enumerate(bits):
                if n > 0:
                    for m in held:
                        begin(None, across(s, m ^ bit, bit))
                fresh = [m ^ bit for m in held]
                for m in fresh:
                    across_in(s, m, bit).wait_recv()
                    begin(None, to_core(s, m))
                    if halo:
                        send_layer(s, m)
                held = held + fresh

        def finish_own(s):
            for m in masks:
                to_core_in(s, m).wait_recv()

        def finish_halo(s):
            for side in (1, -1):
                made = [
                    halo_to_core(s, side, m, me ^ 1 ^ m)
                    for m in masks
                    if cut(arriving(s, side), me ^ 1 ^ m)
                ]

                @pl.when(may_take[side])
                def _():
                    for one in made:
                        one.wait_recv()

        start_gather("y")
        start_gather("z")
        send_layer("y", 0)
        gather("y", True)
        send_layer("z", 0)
        take_direct("y", 0)
        gather("z", True)
        for m in masks[1:]:
            take_direct("y", m)
        for s in ("y", "z"):
            finish_own(s)
        finish_halo("y")
        yield
        start_gather("u")
        send_layer("u", 0)
        for m in masks:
            take_direct("z", m)
        gather("u", True)
        for m in masks:
            take_relayed("z", m)
        finish_own("u")
        finish_halo("z")
        yield
        for m in masks:
            take_direct("u", m)
        for m in masks:
            take_relayed("u", m)
        finish_halo("u")
        yield
        for guard, made in remote:
            if guard is None:
                made.wait_send()
            else:
                pl.when(guard)(made.wait_send)
        yield

    plans = [schedule(me) for me in range(reps)]

    def advance():
        for me in range(reps):
            pl.when(rep == me)(functools.partial(next, plans[me]))

    down = lax.broadcasted_iota(jnp.int32, (tile, tile), 0)
    right = lax.broadcasted_iota(jnp.int32, (tile, tile), 1)
    identity = jnp.where(down == right, 1.5, 0.0).astype(jnp.float32)

    def multiply(left, right, store):
        def step(i, _):
            total = product_row(i, left, right, layer, rep, layers, rows, slots, band)
            for w in range(slots):
                store(i, w, pattern[i, w] == 1, total[:, w * tile : (w + 1) * tile])
            return 0

        lax.fori_loop(0, rows, step, 0)

    def store_update(i, w, good, value):
        value = -0.5 * value + jnp.where(rep * slots + w == half, identity, 0.0)
        u_wide[rows + i, rep * slots + w] = jnp.where(good, value, 0.0).astype(jnp.bfloat16)

    def store_inverse(i, w, good, value):
        z_next[i, w] = jnp.where(good, value, 0.0).astype(jnp.bfloat16)

    def store_square(i, w, good, value):
        y_next[i, w] = jnp.where(good, value, 0.0).astype(jnp.bfloat16)

    advance()
    multiply(z_wide, y_wide, store_update)
    advance()
    multiply(u_wide, z_wide, store_inverse)
    advance()
    multiply(y_wide, u_wide, store_square)
    advance()
    assert len(keys) <= send_sems.shape[0]


def product_row(i, left, right, layer, rep, layers, rows, slots, band):
    half = band // 2
    step = 4
    total = None
    for first in range(0, band, step):
        wide = jnp.concatenate([left[rows + i, u] for u in range(first, first + step)], axis=1)
        tall = []
        for u in range(first, first + step):
            row = layer * rows + i - half + u
            inside = jnp.logical_and(row >= 0, row < layers * rows)
            tiles = []
            for w in range(slots):
                v = rep * slots + w + half - u
                good = jnp.logical_and(inside, jnp.logical_and(v >= 0, v < band))
                part = right[i + u + rows - half, lax.rem(v + band, band)]
                tiles.append(jnp.where(good, part, jnp.zeros_like(part)))
            tall.append(jnp.concatenate(tiles, axis=1))
        piece = jnp.dot(wide, jnp.concatenate(tall, axis=0), preferred_element_type=jnp.float32)
        total = piece if total is None else total + piece
    return total


def solution(mesh):
    layers, reps = mesh.shape["layer"], mesh.shape["rep"]

    def body(inverse_root, square_root, pattern):
        rows, slots = pattern.shape
        tile = inverse_root.shape[2:]
        local = jax.ShapeDtypeStruct((rows, slots) + tile, jnp.bfloat16)
        wide = pltpu.VMEM((3 * rows, slots * reps) + tile, jnp.bfloat16)
        return pl.pallas_call(
            functools.partial(step_kernel, layers, reps, (rows, slots, tile[0])),
            out_shape=(local, local),
            in_specs=[SMEM, VMEM, VMEM],
            out_specs=(VMEM, VMEM),
            scratch_shapes=[
                wide,
                wide,
                wide,
                pltpu.SemaphoreType.DMA((SEMAPHORES,)),
                pltpu.SemaphoreType.DMA((SEMAPHORES,)),
            ],
            compiler_params=pltpu.CompilerParams(
                collective_id=0, has_side_effects=True, vmem_limit_bytes=60 * 1024 * 1024
            ),
            name="newton_step",
        )(pattern, inverse_root, square_root)

    placed = P("layer", "rep", None, None)
    return jax.shard_map(
        body,
        mesh=mesh,
        in_specs=(placed, placed, P("layer", "rep")),
        out_specs=(placed, placed),
        check_vma=False,
    )
```

time: 193 us -> 145 us (0.75)
  the two profiles are of different devices: /device:TPU:17 before, /device:TPU:6 now
where the time goes in v2:
time: 145 us
  Pallas kernels  139 us (96%)
  local copies, waits for them, and re-layouts  4.72 us (3%)
    pallas_call x1, Pallas kernels, body(): pl.pallas_call(functools.partial(step_kernel, layers, reps, (rows, slots,...  139 us
    unnamed x5, local copies, waits for them, and re-layouts  4.72 us

profile of v2, /device:TPU:6, one launch (start us, length us, event | category | flops | bytes accessed | tf_op | source)
XLA Modules:
  0.0 144.6 jit_solution(17228904135822850604)
XLA Ops:
  0.6 1.3 copy.5.pattern
  2.0 139.2 %newton_step.1 = (bf16[8,4,128,128]{3,2,1,0:T(8,128)(2,1)}, bf16[8,4,128,128]{3,2,1,0:T(8,128)(2,1)}) custom-call(s32[8,4]{1,0:T(8,128)} %copy.5.pattern, bf16[8,4,128,128]{3,2,1,0:T(8,128)(2,1)} %z_own.1, bf16[8,4,128,128]{3,2,1,0:T(8,128)(2,1)} %y_own.1), custom_call_target="tpu_custom_call" | custom-call | tf_op jit(solution)/shard_map/newton_step/pallas_call | solution.py:356
  141.2 0.0 copy-start
  141.2 2.4 %copy.8 = bf16[8,4,128,128]{3,2,1,0:T(8,128)(2,1)} copy(bf16[8,4,128,128]{3,2,1,0:T(8,128)(2,1)} %get-tuple-element.4) | data formatting | bytes 2097152
  143.6 0.0 copy-done
  143.6 1.0 copy.9
Async XLA Ops:
  141.2 2.4 %copy-start = (bf16[8,4,128,128]{3,2,1,0:T(8,128)(2,1)S(1)}, bf16[8,4,128,128]{3,2,1,0:T(8,128)(2,1)}, u32[]{:S(2)}) copy-start(bf16[8,4,128,128]{3,2,1,0:T(8,128)(2,1)} %get-tuple-element.5) | copy-start | bytes 3145732
